TPU v7x, 32 devices: a whole 2x2x4 slice. The times are simulated.
32 devices in a mesh: dp: 8 (over y, x, core), mp: 4 (over z).
Axes of the slice: x: 2, y: 2, z: 4, core: 2. Of those that a mesh axis runs over, the one named last changes fastest.
Arguments:
- tokens: bfloat16 [16384, 1024], P(('dp', 'mp')), may hold values from -6 to 6
- norm_gain: float32 [2, 1024], replicated, may hold values from 0.1 to 1.9
- qkv_weight: bfloat16 [3, 1024, 1024], P(None, 'dp', 'mp')
- out_weight: bfloat16 [1024, 1024], P('mp', 'dp'), may hold values from -0.1875 to 0.1875
- variate_bias: float32 [2, 16], replicated, may hold values from -6 to 6
- ffn_weight: bfloat16 [2, 1024, 2816], P(None, 'dp', 'mp'), may hold values from -0.1875 to 0.1875
- down_weight: bfloat16 [2816, 1024], P('mp', 'dp'), may hold values from -0.109375 to 0.109375
- sample_ids: int32 [16384], P(('dp', 'mp')), may hold values from 0 to 127, as said below
- variate_ids: int32 [16384], P(('dp', 'mp')), may hold values from 0 to 15, as said below
- time_ids: int32 [16384], P(('dp', 'mp')), may hold values from 0 to 31, as said below
Outputs:
- encoded: bfloat16 [16384, 1024], P(('dp', 'mp'))
Inputs may be any that keep to these rules, and one draw needn't show every extreme that they name: `sample_ids`: within each packed sequence of 512 tokens the series numbers start at 0 and never fall; a series with v variates (1 to 16) and p patches (4 to 32) holds v * p consecutive tokens, the last series of a sequence may be cut short; some packed sequence holds 128 series of one variate and four patches each. `variate_ids`: A token's offset within its series divided by that series' patch count p. `time_ids`: A token's offset within its series modulo that series' patch count p.
All inputs are finite; a program needn't handle non-finite values.
Results may differ from a plain program's by a relative error of at most 0.017.
Values may be sent and summed in bfloat16 or wider, within the bound.
A program may use at most 128 MiB of HBM per device.

v0:
```python
import jax
import jax.numpy as jnp
from jax import lax
from jax.sharding import PartitionSpec as P

HEAD_DIM = 64
L = 512


def rms_norm(values, gain):
    wide = values.astype(jnp.float32)
    square = jnp.mean(wide * wide, axis=-1, keepdims=True)
    return (wide * lax.rsqrt(square + 1e-05) * gain[None, :]).astype(jnp.bfloat16)


def rotate(values, times):
    half = values.shape[-1] // 2
    freq = 10000.0 ** (-jnp.arange(half, dtype=jnp.float32) / half)
    angle = times.astype(jnp.float32)[:, None] * freq[None, :]
    cosine = jnp.cos(angle)[:, None, :]
    sine = jnp.sin(angle)[:, None, :]
    first = values[..., :half]
    second = values[..., half:]
    return jnp.concatenate(
        [first * cosine - second * sine, first * sine + second * cosine], axis=-1
    )


def rotated(raw, times):
    row_total, local_width = raw.shape
    turned = rotate(raw.reshape(row_total, local_width // HEAD_DIM, HEAD_DIM), times)
    return turned.reshape(row_total, local_width).astype(jnp.bfloat16)


def attend(queries, keys_rot, values, samples, variates, bias):
    row_total, local_width = queries.shape
    heads_here = local_width // HEAD_DIM
    count = row_total // L

    def one_sequence(args):
        qs, ks, vs, sample_row, variate_row = args
        scores = jnp.einsum(
            "qhd,khd->hqk", qs, ks, preferred_element_type=jnp.float32
        ) * HEAD_DIM ** (-0.5)
        same = variate_row[:, None] == variate_row[None, :]
        scores = scores + jnp.where(same[None], bias[0][:, None, None], bias[1][:, None, None])
        scores = jnp.where((sample_row[:, None] == sample_row[None, :])[None], scores, -1e30)
        top = jnp.max(scores, axis=2, keepdims=True)
        expo = jnp.exp(scores - top)
        weights = (expo / jnp.sum(expo, axis=2, keepdims=True)).astype(jnp.bfloat16)
        return jnp.einsum("hqk,khd->qhd", weights, vs, preferred_element_type=jnp.float32).astype(
            jnp.bfloat16
        )

    shape = (count, L, heads_here, HEAD_DIM)
    result = lax.map(
        one_sequence,
        (
            queries.reshape(shape),
            keys_rot.reshape(shape),
            values.reshape(shape),
            samples.reshape(count, L),
            variates.reshape(count, L),
        ),
    )
    return result.reshape(row_total, local_width)


def local(
    tokens,
    norm_gain,
    qkv_weight,
    out_weight,
    variate_bias,
    ffn_weight,
    down_weight,
    sample_ids,
    variate_ids,
    time_ids,
):
    heads_here = qkv_weight.shape[2] // HEAD_DIM
    head_start = lax.axis_index("mp") * heads_here
    bias_local = lax.dynamic_slice_in_dim(variate_bias, head_start, heads_here, 1)
    first_normed = rms_norm(tokens, norm_gain[0])
    wide_columns = lax.all_gather(qkv_weight, "mp", axis=2, tiled=True)
    columns = first_normed
    projected = jnp.einsum(
        "rc,jcd->jrd",
        columns,
        lax.all_gather(wide_columns, "dp", axis=1, tiled=True),
        preferred_element_type=jnp.float32,
    )
    queries = rotated(projected[0], time_ids)
    keys_rot = rotated(projected[1], time_ids)
    values = projected[2].astype(jnp.bfloat16)
    grouped = lax.all_to_all(
        jnp.stack([queries, keys_rot, values]), "mp", split_axis=2, concat_axis=1, tiled=True
    )
    gathered_ids = (
        lax.all_gather(sample_ids, "mp", axis=0, tiled=True),
        lax.all_gather(variate_ids, "mp", axis=0, tiled=True),
    )
    attended = attend(
        grouped[0], grouped[1], grouped[2], gathered_ids[0], gathered_ids[1], bias_local
    )
    back_rows = lax.all_to_all(attended, "mp", split_axis=0, concat_axis=1, tiled=True)
    out_rows = lax.all_gather(out_weight, "mp", axis=0, tiled=True)
    mixed = jnp.dot(
        back_rows,
        lax.all_gather(out_rows, "dp", axis=1, tiled=True),
        preferred_element_type=jnp.float32,
    )
    residual = (tokens.astype(jnp.float32) + mixed).astype(jnp.bfloat16)
    second_normed = rms_norm(residual, norm_gain[1])
    ffn_columns = lax.all_gather(ffn_weight, "mp", axis=2, tiled=True)
    columns = second_normed
    gate_up = jnp.einsum(
        "rc,jcf->jrf",
        columns,
        lax.all_gather(ffn_columns, "dp", axis=1, tiled=True),
        preferred_element_type=jnp.float32,
    )
    hidden = (jax.nn.silu(gate_up[0]) * gate_up[1]).astype(jnp.bfloat16)
    down_full = lax.all_gather(down_weight, "mp", axis=0, tiled=True)
    feed = jnp.dot(
        hidden,
        lax.all_gather(down_full, "dp", axis=1, tiled=True),
        preferred_element_type=jnp.float32,
    )
    return (residual.astype(jnp.float32) + feed).astype(jnp.bfloat16)


def solution(mesh):
    return jax.shard_map(
        local,
        mesh=mesh,
        in_specs=(
            P(("dp", "mp"), None),
            P(),
            P(None, "dp", "mp"),
            P("mp", "dp"),
            P(),
            P(None, "dp", "mp"),
            P("mp", "dp"),
            P(("dp", "mp")),
            P(("dp", "mp")),
            P(("dp", "mp")),
        ),
        out_specs=P(("dp", "mp"), None),
        check_vma=False,
    )
```

profile of v0, /device:TPU:0, one launch (start us, length us, event | category | flops | bytes accessed | tf_op | source)
XLA Modules:
  0.0 358.3 jit_solution(14907393396261247635)
XLA Ops:
  6.5 2.2 copy.40
  8.8 27.7 %all_gather.30 = bf16[3,128,1024]{2,1,0:T(8,128)(2,1)} all-gather(bf16[3,128,256]{2,1,0:T(8,128)(2,1)} %param.14), channel_id=1, replica_groups=mesh['dp'=8,'mp'=4] {'mp'}, dimensions={2}, use_global_device_ids=true | all-gather | bytes 983040 | tf_op jit(solution)/shard_map/all_gather | solution.py:85
  36.6 18.9 %all_gather.34 = bf16[1024,128]{1,0:T(8,128)(2,1)} all-gather(bf16[256,128]{1,0:T(8,128)(2,1)} %param.15), channel_id=1, replica_groups=mesh['dp'=8,'mp'=4] {'mp'}, dimensions={0}, use_global_device_ids=true | all-gather | bytes 327680 | tf_op jit(solution)/shard_map/all_gather | solution.py:107
  55.5 1.2 all-gather.12.cloned.1.call-done
  56.8 4.9 %copy.41 = bf16[2,128,2816]{2,1,0:T(8,128)(2,1)} copy(bf16[2,128,2816]{1,0,2:T(2,128)(2,1)} %all-gather.12.cloned.1.call-done) | data formatting | bytes 2883584 | tf_op jit(solution)/shard_map/all_gather | solution.py:115
  61.7 0.3 fusion.56
  62.0 0.3 multiply_cosine_fusion
  62.3 41.2 %all-gather.8.cloned.1.call-done = bf16[3,1024,1024]{2,1,0:T(8,128)(2,1)} async-done(((bf16[3,128,1024]{2,1,0:T(8,128)(2,1)}), bf16[3,1024,1024]{2,1,0:T(8,128)(2,1)}) %all-gather.8.cloned.1.call-update) | async-done | bytes 6291472 | tf_op jit(solution)/shard_map/all_gather | solution.py:90
  103.5 5.7 %convolution_bitcast_fusion.1 = f32[3,512,1024]{2,1,0:T(8,128)S(1)} fusion(bf16[3,1024,1024]{2,1,0:T(8,128)(2,1)} %all-gather.8.cloned.1.call-done, bf16[512,1024]{1,0:T(8,128)(2,1)S(1)} %copy-done.2, f32[1024]{0:T(1024)S(1)} %bitcast.128, f32[512]{0:T(512)S(1)} %add_rsqrt_fusion.1), kind=kOutput, calls=%fused_computation.54 | convolution fusion | flops 3223322624 | bytes 13637632 | tf_op jit(solution)/shard_map/rc,jcd->jrd/dot_general | solution.py:87
  109.3 1.1 slice.103
  110.4 2.4 fusion.80
  112.8 2.0 copy.34
  114.8 2.9 copy.35
  117.7 2.3 subtract_convert_fusion.1
  120.0 0.1 pad_maximum_fusion.1
  120.1 1.3 copy.36
  121.5 1.3 copy.37
  122.8 2.5 pad_maximum_fusion
  125.3 5.7 %copy.38 = bf16[3,512,1024]{1,0,2:T(4,128)(2,1)} copy(bf16[3,512,1024]{2,1,0:T(8,128)(2,1)S(1)} %pad_maximum_fusion) | data formatting | bytes 6291456 | tf_op jit(solution)/shard_map/stack | solution.py:97
  131.0 5.0 %all-to-all-start = ((bf16[3,512,1024]{1,0,2:T(4,128)(2,1)}), bf16[3,512,1024]{1,0,2:T(4,128)(2,1)}, u32[]{:S(2)}, u32[]{:S(2)}) async-start(bf16[3,512,1024]{1,0,2:T(4,128)(2,1)} %copy.38), calls=%async_computation | async-start | bytes 8388608 | tf_op jit(solution)/shard_map/all_to_all | solution.py:96
  136.1 106.7 %all_gather.38 = bf16[2816,128]{1,0:T(8,128)(2,1)} all-gather(bf16[704,128]{1,0:T(8,128)(2,1)S(1)} %copy-done.4), channel_id=1, replica_groups=mesh['dp'=8,'mp'=4] {'mp'}, dimensions={0}, use_global_device_ids=true | all-gather | bytes 901120 | tf_op jit(solution)/shard_map/all_gather | solution.py:124
  242.9 11.9 %all-gather.1 = s32[4,1,512]{2,1,0:T(1,128)S(1)} all-gather(s32[1,1,512]{2,1,0:T(1,128)S(1)} %bitcast.129), channel_id=1, replica_groups=mesh['dp'=8,'mp'=4] {'mp'}, dimensions={0}, use_global_device_ids=true | all-gather | bytes 10240 | tf_op jit(solution)/shard_map/all_gather | solution.py:101
  254.8 12.1 %all-gather = s32[4,1,512]{2,1,0:T(1,128)S(1)} all-gather(s32[1,1,512]{2,1,0:T(1,128)S(1)} %bitcast.130), channel_id=1, replica_groups=mesh['dp'=8,'mp'=4] {'mp'}, dimensions={0}, use_global_device_ids=true | all-gather | bytes 10240 | tf_op jit(solution)/shard_map/all_gather | solution.py:100
  266.9 0.1 constant_dynamic-slice_fusion.2
  267.0 3.2 copy.39
  270.2 1.5 fusion.81
  271.7 31.2 %while.10 = (s32[]{:T(128)}, bf16[4,512,4,64]{1,3,2,0:T(8,128)(2,1)}, bf16[4,512,4,64]{1,3,2,0:T(8,128)(2,1)}, s32[4,512]{1,0:T(4,128)S(1)}, bf16[4,512,4,64]{1,...) while((s32[]{:T(128)}, ...), condition=%wide.region_4.5_spmd, body=%wide.region_1.4_spmd.sunk | while | flops 416943104 | bytes 3179681 | solution.py:56
  271.7 0.2 broadcast_compare_fusion.4
  271.9 0.2 broadcast_compare_fusion.5
  272.2 3.0 fusion.100
  275.2 4.3 %fusion.101 = bf16[4,512,4,64]{1,3,2,0:T(8,128)(2,1)} fusion(bf16[4,512,4,64]{1,3,2,0:T(8,128)(2,1)} %get-tuple-element.154, s32[]{:T(128)} %get-tuple-element.153, f32[4,512]{1,0:T(4,128)S(1)} %fusion.100, bf16[4,512,4,64]{1,3,2,0:T(8,128)(2,1)} %get-tuple-element.164, f32[4]{0:T(128)S(1)} %get-tuple-element.140, f32[4]{0:T(128)S(1)} %get-tuple-element.141, ...), kind=kOutput, calls=%fused_computation.14.clone.1 | convolution fusion | flops 275909120 | bytes 1584128 | tf_op jit(solution)/shard_map/while/body/eval_jaxpr/hqk,khd->qhd/dot_general | solution.py:51
  279.5 0.2 broadcast_compare_fusion.4
  279.7 0.2 broadcast_compare_fusion.5
  280.0 3.0 fusion.100
  283.0 4.3 %fusion.101 = bf16[4,512,4,64]{1,3,2,0:T(8,128)(2,1)} fusion(bf16[4,512,4,64]{1,3,2,0:T(8,128)(2,1)} %get-tuple-element.154, s32[]{:T(128)} %get-tuple-element.153, f32[4,512]{1,0:T(4,128)S(1)} %fusion.100, bf16[4,512,4,64]{1,3,2,0:T(8,128)(2,1)} %get-tuple-element.164, f32[4]{0:T(128)S(1)} %get-tuple-element.140, f32[4]{0:T(128)S(1)} %get-tuple-element.141, ...), kind=kOutput, calls=%fused_computation.14.clone.1 | convolution fusion | flops 275909120 | bytes 1584128 | tf_op jit(solution)/shard_map/while/body/eval_jaxpr/hqk,khd->qhd/dot_general | solution.py:51
  287.3 0.2 broadcast_compare_fusion.4
  287.5 0.2 broadcast_compare_fusion.5
  287.8 3.0 fusion.100
  290.8 4.3 %fusion.101 = bf16[4,512,4,64]{1,3,2,0:T(8,128)(2,1)} fusion(bf16[4,512,4,64]{1,3,2,0:T(8,128)(2,1)} %get-tuple-element.154, s32[]{:T(128)} %get-tuple-element.153, f32[4,512]{1,0:T(4,128)S(1)} %fusion.100, bf16[4,512,4,64]{1,3,2,0:T(8,128)(2,1)} %get-tuple-element.164, f32[4]{0:T(128)S(1)} %get-tuple-element.140, f32[4]{0:T(128)S(1)} %get-tuple-element.141, ...), kind=kOutput, calls=%fused_computation.14.clone.1 | convolution fusion | flops 275909120 | bytes 1584128 | tf_op jit(solution)/shard_map/while/body/eval_jaxpr/hqk,khd->qhd/dot_general | solution.py:51
  295.1 0.2 broadcast_compare_fusion.4
  295.4 0.2 broadcast_compare_fusion.5
  295.6 3.0 fusion.100
  298.6 4.3 %fusion.101 = bf16[4,512,4,64]{1,3,2,0:T(8,128)(2,1)} fusion(bf16[4,512,4,64]{1,3,2,0:T(8,128)(2,1)} %get-tuple-element.154, s32[]{:T(128)} %get-tuple-element.153, f32[4,512]{1,0:T(4,128)S(1)} %fusion.100, bf16[4,512,4,64]{1,3,2,0:T(8,128)(2,1)} %get-tuple-element.164, f32[4]{0:T(128)S(1)} %get-tuple-element.140, f32[4]{0:T(128)S(1)} %get-tuple-element.141, ...), kind=kOutput, calls=%fused_computation.14.clone.1 | convolution fusion | flops 275909120 | bytes 1584128 | tf_op jit(solution)/shard_map/while/body/eval_jaxpr/hqk,khd->qhd/dot_general | solution.py:51
  302.9 3.7 %all-to-all-start.1 = ((bf16[4,512,256]{1,2,0:T(8,128)(2,1)}), bf16[4,512,256]{1,2,0:T(8,128)(2,1)S(1)}, u32[]{:S(2)}, u32[]{:S(2)}) async-start(bf16[4,512,256]{1,2,0:T(8,128)(2,1)} %bitcast.24), calls=%async_computation.1 | async-start | bytes 2097152 | tf_op jit(solution)/shard_map/all_to_all | solution.py:106
  306.7 18.6 %all-to-all-done.1 = bf16[4,512,256]{1,2,0:T(8,128)(2,1)S(1)} async-done(((bf16[4,512,256]{1,2,0:T(8,128)(2,1)}), bf16[4,512,256]{1,2,0:T(8,128)(2,1)S(1)}, u32[]{:S(2)}, u32[]{:S(2)}) %all-to-all-start.1) | async-done | bytes 1048608 | tf_op jit(solution)/shard_map/all_to_all | solution.py:106
  325.3 3.0 fusion.60
  328.3 13.2 %convolution_bitcast_fusion = f32[2,512,2816]{2,1,0:T(8,128)} fusion(bf16[2,1024,2816]{2,1,0:T(8,128)(2,1)} %all-gather.14.cloned.1.call-done, bf16[512,1024]{1,0:T(8,128)(2,1)S(1)} %get-tuple-element.84, f32[1024]{0:T(1024)S(1)} %bitcast.125, f32[512]{0:T(512)S(1)} %add_rsqrt_fusion), kind=kOutput, calls=%fused_computation.41 | convolution fusion | flops 5907677184 | bytes 24123392 | tf_op jit(solution)/shard_map/rc,jcf->jrf/dot_general | solution.py:117
  341.6 10.2 %fusion.63 = bf16[512,1024]{1,0:T(8,128)(2,1)} fusion(bf16[512,1024]{1,0:T(8,128)(2,1)S(1)} %get-tuple-element.84, bf16[2816,1024]{1,0:T(8,128)(2,1)} %all-gather.16.cloned.1.call-done, f32[2,512,2816]{2,1,0:T(8,128)} %convolution_bitcast_fusion), kind=kOutput, calls=%fused_computation.62 | convolution fusion | flops 2963013632 | bytes 19398656 | tf_op jit(solution)/shard_map/dot_general | solution.py:125
  (48 shorter events, 0.4 us)
Async XLA Ops:
  6.5 260.4 %copy-start = (f32[2,16]{1,0:T(2,128)S(1)}, f32[2,16]{1,0:T(2,128)}, u32[]{:S(2)}) copy-start(f32[2,16]{1,0:T(2,128)} %param.16) | copy-start | bytes 388
  6.5 55.1 %copy-start.8 = (s32[512]{0:T(512)S(1)}, s32[512]{0:T(512)}, u32[]{:S(2)}) copy-start(s32[512]{0:T(512)} %param.21) | copy-start | bytes 6148
  6.5 55.2 %copy-start.2 = (bf16[512,1024]{1,0:T(8,128)(2,1)S(1)}, bf16[512,1024]{1,0:T(8,128)(2,1)}, u32[]{:S(2)}) copy-start(bf16[512,1024]{1,0:T(8,128)(2,1)} %param.12) | copy-start | bytes 3145732
  6.5 50.2 %all-gather.12.cloned.1.call-start = ((), (), s32[]{:S(2)}) async-start(), calls=%async_computation.4 | async-start | bytes 1802240 | tf_op jit(solution)/shard_map/all_gather | solution.py:115
  8.7 53.3 %copy-start.5 = (f32[2,1024]{1,0:T(2,128)S(1)}, f32[2,1024]{1,0:T(2,128)}, u32[]{:S(2)}) copy-start(f32[2,1024]{1,0:T(2,128)} %param.13) | copy-start | bytes 24580
  8.8 94.8 %all-gather.8.cloned.1.call-start = ((), (), s32[]{:S(2)}) async-start(), calls=%async_computation.2 | async-start | bytes 7077888 | tf_op jit(solution)/shard_map/all_gather | solution.py:90
  36.5 270.2 %all-gather.10.cloned.1.call-start = ((), (), s32[]{:S(2)}) async-start(), calls=%async_computation.3 | async-start | bytes 2359296 | tf_op jit(solution)/shard_map/all_gather | solution.py:110
  55.5 272.8 %all-gather.14.cloned.1.call-start = ((), (), s32[]{:S(2)}) async-start(), calls=%async_computation.5 | async-start | bytes 12976128 | tf_op jit(solution)/shard_map/all_gather | solution.py:120
  131.0 5.1 %copy-start.4 = (bf16[704,128]{1,0:T(8,128)(2,1)S(1)}, bf16[704,128]{1,0:T(8,128)(2,1)}, u32[]{:S(2)}) copy-start(bf16[704,128]{1,0:T(8,128)(2,1)} %param.18) | copy-start | bytes 540676
  131.0 111.8 %copy-start.6 = (s32[512]{0:T(512)S(1)}, s32[512]{0:T(512)}, u32[]{:S(2)}) copy-start(s32[512]{0:T(512)} %param.20) | copy-start | bytes 6148
  131.0 123.8 %copy-start.7 = (s32[512]{0:T(512)S(1)}, s32[512]{0:T(512)}, u32[]{:S(2)}) copy-start(s32[512]{0:T(512)} %param.19) | copy-start | bytes 6148
  131.0 136.0 %all-to-all-start = ((bf16[3,512,1024]{1,0,2:T(4,128)(2,1)}), bf16[3,512,1024]{1,0,2:T(4,128)(2,1)}, u32[]{:S(2)}, u32[]{:S(2)}) async-start(bf16[3,512,1024]{1,0,2:T(4,128)(2,1)} %copy.38), calls=%async_computation | async-start | bytes 8388608 | tf_op jit(solution)/shard_map/all_to_all | solution.py:96
  136.0 205.6 %all-gather.16.cloned.1.call-start = ((), (), s32[]{:S(2)}) async-start(), calls=%async_computation.6 | async-start | bytes 6488064 | tf_op jit(solution)/shard_map/all_gather | solution.py:127
  271.7 53.6 %copy-start.3 = (bf16[512,1024]{1,0:T(8,128)(2,1)S(1)}, bf16[512,1024]{1,0:T(8,128)(2,1)}, u32[]{:S(2)}) copy-start(bf16[512,1024]{1,0:T(8,128)(2,1)} %param.12) | copy-start | bytes 3145732
  302.9 22.3 %all-to-all-start.1 = ((bf16[4,512,256]{1,2,0:T(8,128)(2,1)}), bf16[4,512,256]{1,2,0:T(8,128)(2,1)S(1)}, u32[]{:S(2)}, u32[]{:S(2)}) async-start(bf16[4,512,256]{1,2,0:T(8,128)(2,1)} %bitcast.24), calls=%async_computation.1 | async-start | bytes 2097152 | tf_op jit(solution)/shard_map/all_to_all | solution.py:106
  341.6 10.2 %copy-start.1 = (f32[2,16]{1,0:T(2,128)S(1)}, f32[2,16]{1,0:T(2,128)}, u32[]{:S(2)}) copy-start(f32[2,16]{1,0:T(2,128)} %param.16) | copy-start | bytes 388
Sparse Core Ops, SparseCore 0:
  8.9 47.8 all-gather.11
  58.7 44.7 all-gather.7
  105.4 28.0 all-gather.9
  135.3 67.5 all-gather.13
  243.0 44.4 all-gather.15
where the time goes:
time: 359 us; the launch traced here: 358 us
  blocking collectives  177 us (49%)
  matrix products  61.5 us (17%)
  waiting for transfers between devices  61.1 us (17%)
  local copies, waits for them, and re-layouts  28.7 us (8%)
  between operations  13.3 us (4%)
  starting transfers between devices  8.9 us (2%)
  other arithmetic  7.24 us (2%)
    all_gather x1, blocking collectives, local(): down_full = lax.all_gather(down_weight, 'mp', axis=0, tiled=True)  107 us
    all_gather x1, waiting for transfers between devices, local(): lax.all_gather(wide_columns, 'dp', axis=1, tiled=True)  41.2 us
    all_gather x1, blocking collectives, local(): wide_columns = lax.all_gather(qkv_weight, 'mp', axis=2, tiled=True)  27.7 us
    all_gather x1, blocking collectives, local(): out_rows = lax.all_gather(out_weight, 'mp', axis=0, tiled=True)  18.9 us
    all_to_all x1, waiting for transfers between devices, local(): lax.all_to_all(attended, 'mp', split_axis=0, concat_axis=1, tiled=True)  18.6 us
    dot_general x4, matrix products, one_sequence(): jnp.einsum('hqk,khd->qhd', weights, vs, preferred_element_type=jnp.float32)  17.2 us
    dot_general x1, matrix products, local(): jnp.einsum('rc,jcf->jrf', columns, lax.all_gather(ffn_columns, 'dp', axis...  13.2 us
    sub x4, matrix products, one_sequence(): expo = jnp.exp(scores - top)  12.1 us
  transfers between devices with their start and end apart: 7, of which 3 were waited for; matrix products, arithmetic and copies ran while one was open for 24% of the time, Pallas kernels for 0%

commit v1 on v0

--- a/solution.py
+++ b/solution.py
@@ -78,9 +78,6 @@
     variate_ids,
     time_ids,
 ):
-    heads_here = qkv_weight.shape[2] // HEAD_DIM
-    head_start = lax.axis_index("mp") * heads_here
-    bias_local = lax.dynamic_slice_in_dim(variate_bias, head_start, heads_here, 1)
     first_normed = rms_norm(tokens, norm_gain[0])
     wide_columns = lax.all_gather(qkv_weight, "mp", axis=2, tiled=True)
     columns = first_normed
@@ -93,17 +90,7 @@
     queries = rotated(projected[0], time_ids)
     keys_rot = rotated(projected[1], time_ids)
     values = projected[2].astype(jnp.bfloat16)
-    grouped = lax.all_to_all(
-        jnp.stack([queries, keys_rot, values]), "mp", split_axis=2, concat_axis=1, tiled=True
-    )
-    gathered_ids = (
-        lax.all_gather(sample_ids, "mp", axis=0, tiled=True),
-        lax.all_gather(variate_ids, "mp", axis=0, tiled=True),
-    )
-    attended = attend(
-        grouped[0], grouped[1], grouped[2], gathered_ids[0], gathered_ids[1], bias_local
-    )
-    back_rows = lax.all_to_all(attended, "mp", split_axis=0, concat_axis=1, tiled=True)
+    back_rows = attend(queries, keys_rot, values, sample_ids, variate_ids, variate_bias)
     out_rows = lax.all_gather(out_weight, "mp", axis=0, tiled=True)
     mixed = jnp.dot(
         back_rows,

time: 359 us -> 266 us (0.74)
  blocking collectives: 177 us -> 64.8 us
  waiting for transfers between devices: 61.1 us -> 114 us
  local copies, waits for them, and re-layouts: 28.7 us -> 15.9 us
  starting transfers between devices: 8.9 us -> 0.21 us
  matrix products: 61.5 us -> 53 us
    all_gather x1, blocking collectives: 107 us -> 18.1 us  [local(): down_full = lax.all_gather(down_weight, 'mp', axis=0, tiled=True)]
    all_gather x1, waiting for transfers between devices: 0.02 us -> 57.8 us  [local(): lax.all_gather(ffn_columns, 'dp', axis=1, tiled=True)]
    all_gather x1, waiting for transfers between devices: 0.01 us -> 32.7 us  [local(): lax.all_gather(down_full, 'dp', axis=1, tiled=True)]
    all_gather x2 -> x0, blocking collectives: 24 us -> none  [the longest x1 12.1 us: local(): lax.all_gather(sample_ids, 'mp', axis=0, tiled=True)]
    all_gather x1, waiting for transfers between devices: 41.2 us -> 21.9 us  [local(): lax.all_gather(wide_columns, 'dp', axis=1, tiled=True)]
    all_to_all x2 -> x0, waiting for transfers between devices: 18.6 us -> none  [the longest x1 18.6 us: local(): lax.all_to_all(attended, 'mp', split_axis=0, concat_axis=1, tiled=True)]
    all_to_all x2 -> x0, starting transfers between devices: 8.73 us -> none  [the longest x1 4.99 us: local(): lax.all_to_all(jnp.stack([queries, keys_rot, values]), 'mp', split_axis=2...]
    dot_general x4 -> x1, matrix products: 17.2 us -> 11.1 us  [one_sequence(): jnp.einsum('hqk,khd->qhd', weights, vs, preferred_element_type=jnp.float32)]
  transfers between devices with their start and end apart: 7 -> 5, of which waited for: 3 -> 4; matrix products, arithmetic and copies ran while one was open for 24% -> 23% of each run, Pallas kernels for 0% -> 0%
where the time goes in v1:
time: 266 us
  waiting for transfers between devices  114 us (43%)
  blocking collectives  64.8 us (24%)
  matrix products  53 us (20%)
  local copies, waits for them, and re-layouts  15.9 us (6%)
  between operations  13.3 us (5%)
  other arithmetic  4.88 us (2%)
    all_gather x1, waiting for transfers between devices, local(): lax.all_gather(ffn_columns, 'dp', axis=1, tiled=True)  57.8 us
    all_gather x1, waiting for transfers between devices, local(): lax.all_gather(down_full, 'dp', axis=1, tiled=True)  32.7 us
    all_gather x1, blocking collectives, local(): wide_columns = lax.all_gather(qkv_weight, 'mp', axis=2, tiled=True)  27.7 us
    all_gather x1, waiting for transfers between devices, local(): lax.all_gather(wide_columns, 'dp', axis=1, tiled=True)  21.9 us
    all_gather x1, blocking collectives, local(): out_rows = lax.all_gather(out_weight, 'mp', axis=0, tiled=True)  19 us
    all_gather x1, blocking collectives, local(): down_full = lax.all_gather(down_weight, 'mp', axis=0, tiled=True)  18.1 us
    dot_general x1, matrix products, local(): jnp.einsum('rc,jcf->jrf', columns, lax.all_gather(ffn_columns, 'dp', axis...  13.3 us
    dot_general x1, matrix products, one_sequence(): jnp.einsum('hqk,khd->qhd', weights, vs, preferred_element_type=jnp.float32)  11.1 us
  transfers between devices with their start and end apart: 5, of which 4 were waited for; matrix products, arithmetic and copies ran while one was open for 23% of the time, Pallas kernels for 0%

profile of v1, /device:TPU:0, one launch (start us, length us, event | category | flops | bytes accessed | tf_op | source)
XLA Modules:
  0.0 265.7 jit_solution(9024680529559725444)
XLA Ops:
  6.5 0.0 copy-start.3
  6.5 0.0 copy-start.7
  6.5 0.0 copy-start.5
  6.6 0.0 copy-start.4
  6.6 0.0 all-gather.10.cloned.1.call-start
  6.6 2.2 copy.27
  8.8 0.0 all-gather.10.cloned.1.call-update
  8.8 0.0 all-gather.6.cloned.1.call-start
  8.9 27.7 %all_gather.24 = bf16[3,128,1024]{2,1,0:T(8,128)(2,1)} all-gather(bf16[3,128,256]{2,1,0:T(8,128)(2,1)} %param.12), channel_id=1, replica_groups=mesh['dp'=8,'mp'=4] {'mp'}, dimensions={2}, use_global_device_ids=true | all-gather | bytes 983040 | tf_op jit(solution)/shard_map/all_gather | solution.py:82
  36.6 0.0 all-gather.6.cloned.1.call-update
  36.6 0.0 all-gather.8.cloned.1.call-start
  36.7 19.0 %all_gather.26 = bf16[1024,128]{1,0:T(8,128)(2,1)} all-gather(bf16[256,128]{1,0:T(8,128)(2,1)} %param.13), channel_id=1, replica_groups=mesh['dp'=8,'mp'=4] {'mp'}, dimensions={0}, use_global_device_ids=true | all-gather | bytes 327680 | tf_op jit(solution)/shard_map/all_gather | solution.py:94
  55.6 0.0 all-gather.8.cloned.1.call-update
  55.7 0.0 all-gather.12.cloned.1.call-start
  55.7 1.1 all-gather.10.cloned.1.call-done
  56.9 4.9 %copy.28 = bf16[2,128,2816]{2,1,0:T(8,128)(2,1)} copy(bf16[2,128,2816]{1,0,2:T(2,128)(2,1)} %all-gather.10.cloned.1.call-done) | data formatting | bytes 2883584 | tf_op jit(solution)/shard_map/all_gather | solution.py:102
  61.8 0.0 all-gather.12.cloned.1.call-update
  61.8 0.0 all-gather.14.cloned.1.call-start
  61.8 0.0 copy-done.3
  61.8 18.1 %all_gather.30 = bf16[2816,128]{1,0:T(8,128)(2,1)} all-gather(bf16[704,128]{1,0:T(8,128)(2,1)S(1)} %copy-done.3), channel_id=1, replica_groups=mesh['dp'=8,'mp'=4] {'mp'}, dimensions={0}, use_global_device_ids=true | all-gather | bytes 901120 | tf_op jit(solution)/shard_map/all_gather | solution.py:111
  79.9 0.0 all-gather.14.cloned.1.call-update
  79.9 0.0 copy-done.7
  80.0 0.0 copy-done
  80.0 0.3 fusion.15
  80.3 0.0 copy-done.8
  80.3 0.0 copy-done.6
  80.3 0.3 multiply_cosine_fusion
  80.6 0.0 copy-done.5
  80.6 0.0 copy-done.4
  80.6 1.1 broadcast_compare_fusion
  81.7 21.9 %all-gather.6.cloned.1.call-done = bf16[3,1024,1024]{2,1,0:T(8,128)(2,1)} async-done(((bf16[3,128,1024]{2,1,0:T(8,128)(2,1)}), bf16[3,1024,1024]{2,1,0:T(8,128)(2,1)}) %all-gather.6.cloned.1.call-update) | async-done | bytes 6291472 | tf_op jit(solution)/shard_map/all_gather | solution.py:87
  103.6 5.7 %convolution_bitcast_fusion.1 = f32[3,512,1024]{2,1,0:T(8,128)S(1)} fusion(bf16[3,1024,1024]{2,1,0:T(8,128)(2,1)} %all-gather.6.cloned.1.call-done, bf16[512,1024]{1,0:T(8,128)(2,1)S(1)} %copy-done, f32[1024]{0:T(1024)S(1)} %bitcast.48, f32[512]{0:T(512)S(1)} %add_rsqrt_fusion.1), kind=kOutput, calls=%fused_computation.25 | convolution fusion | flops 3223322624 | bytes 13637632 | tf_op jit(solution)/shard_map/rc,jcd->jrd/dot_general | solution.py:84
  109.3 0.2 slice.89
  109.4 2.4 fusion.49
  111.9 2.0 copy.24
  113.8 2.9 %copy.25 = f32[1,512,1024]{1,2,0:T(8,128)} copy(f32[1,512,1024]{2,1,0:T(8,128)} %get-tuple-element.20) | data formatting | bytes 4194304 | tf_op jit(solution)/shard_map/slice | solution.py:91
  116.8 1.3 copy.23
  118.1 3.2 %subtract_convert_fusion.1 = (bf16[512,16,32]{0,2,1:T(8,128)(2,1)S(1)}, bf16[512,16,32]{0,2,1:T(8,128)(2,1)S(1)}, bf16[512,16,32]{0,2,1:T(8,128)(2,1)}, bf16[512,16,32]{0,2,1:T(8,128)(2,1)}) fusion(f32[512,16,64]{0,2,1:T(8,128)S(1)} %bitcast.44, f32[512,32]{0,1:T(8,128)S(1)} %get-tuple-element.40, f32[512,32]{0,1:T(8,128)S(1)} %get-tuple-element.39, ...), kind=kLoop, calls=%fused_computation.45 | loop fusion | flops 4194304 | bytes 6422528 | tf_op jit(solution)/shard_map/convert.2
  121.3 9.0 %fusion.51 = f32[16,512]{1,0:T(8,128)S(1)} fusion(f32[16]{0:T(128)S(1)} %get-tuple-element.42, f32[16]{0:T(128)S(1)} %get-tuple-element.41, pred[512,512]{0,1:T(8,128)(4,1)S(1)} %get-tuple-element.45, pred[512,512]{0,1:T(8,128)(4,1)} %get-tuple-element.46, bf16[512,16,32]{0,2,1:T(8,128)(2,1)} %get-tuple-element.34, ...), kind=kOutput, calls=%fused_computation.69 | convolution fusion | flops 566231552 | bytes 2654336 | tf_op jit(solution)/shard_map/while/body/eval_jaxpr/sub | solution.py:49
  130.3 0.0 copy-done.2
  130.3 0.0 copy-start.1
  130.3 11.1 %fusion.25 = bf16[16,64,512]{2,1,0:T(8,128)(2,1)} fusion(bf16[512,16,64]{0,2,1:T(8,128)(2,1)S(1)} %bitcast.46, f32[16,512]{1,0:T(8,128)S(1)} %fusion.51, f32[16]{0:T(128)S(1)} %get-tuple-element.42, f32[16]{0:T(128)S(1)} %get-tuple-element.41, pred[512,512]{0,1:T(8,128)(4,1)S(1)} %get-tuple-element.45, pred[512,512]{0,1:T(8,128)(4,1)} %get-tuple-element.46, ...), kind=kOutput, calls=%fused_computation.35 | convolution fusion | flops 1107829248 | bytes 4751488 | tf_op jit(solution)/shard_map/while/body/eval_jaxpr/hqk,khd->qhd/dot_general | solution.py:51
  141.4 0.0 copy-done.1
  141.4 3.8 %fusion.19 = (f32[512]{0:T(512)S(1)}, bf16[512,1024]{1,0:T(8,128)(2,1)S(1)}) fusion(bf16[512,1024]{0,1:T(8,128)(2,1)} %bitcast.49, bf16[1024,1024]{1,0:T(8,128)(2,1)} %all-gather.8.cloned.1.call-done, bf16[512,1024]{1,0:T(8,128)(2,1)S(1)} %copy-done.1), kind=kOutput, calls=%fused_computation.30 | convolution fusion | flops 1076887040 | bytes 5244928 | tf_op jit(solution)/shard_map/dot_general | solution.py:95
  145.2 57.8 %all-gather.12.cloned.1.call-done = bf16[2,1024,2816]{2,1,0:T(8,128)(2,1)} async-done(((bf16[2,128,2816]{2,1,0:T(8,128)(2,1)}), bf16[2,1024,2816]{2,1,0:T(8,128)(2,1)}) %all-gather.12.cloned.1.call-update) | async-done | bytes 11534352 | tf_op jit(solution)/shard_map/all_gather | solution.py:107
  202.9 13.3 %convolution_bitcast_fusion = f32[2,512,2816]{2,1,0:T(8,128)} fusion(bf16[2,1024,2816]{2,1,0:T(8,128)(2,1)} %all-gather.12.cloned.1.call-done, bf16[512,1024]{1,0:T(8,128)(2,1)S(1)} %get-tuple-element.44, f32[1024]{0:T(1024)S(1)} %bitcast.47, f32[512]{0:T(512)S(1)} %add_rsqrt_fusion), kind=kOutput, calls=%fused_computation.12 | convolution fusion | flops 5907677184 | bytes 24123392 | tf_op jit(solution)/shard_map/rc,jcf->jrf/dot_general | solution.py:104
  216.2 32.7 %all-gather.14.cloned.1.call-done = bf16[2816,1024]{1,0:T(8,128)(2,1)} async-done(((bf16[2816,128]{1,0:T(8,128)(2,1)}), bf16[2816,1024]{1,0:T(8,128)(2,1)}) %all-gather.14.cloned.1.call-update) | async-done | bytes 5767184 | tf_op jit(solution)/shard_map/all_gather | solution.py:114
  249.0 10.2 %fusion.22 = bf16[512,1024]{1,0:T(8,128)(2,1)} fusion(bf16[512,1024]{1,0:T(8,128)(2,1)S(1)} %get-tuple-element.44, bf16[2816,1024]{1,0:T(8,128)(2,1)} %all-gather.14.cloned.1.call-done, f32[2,512,2816]{2,1,0:T(8,128)} %convolution_bitcast_fusion), kind=kOutput, calls=%fused_computation.33 | convolution fusion | flops 2963013632 | bytes 19398656 | tf_op jit(solution)/shard_map/dot_general | solution.py:112
  (11 shorter events, 0.0 us)
Async XLA Ops:
  6.5 55.3 %copy-start.3 = (bf16[704,128]{1,0:T(8,128)(2,1)S(1)}, bf16[704,128]{1,0:T(8,128)(2,1)}, u32[]{:S(2)}) copy-start(bf16[704,128]{1,0:T(8,128)(2,1)} %param.16) | copy-start | bytes 540676
  6.5 73.4 %copy-start.7 = (s32[512]{0:T(512)S(1)}, s32[512]{0:T(512)}, u32[]{:S(2)}) copy-start(s32[512]{0:T(512)} %param.19) | copy-start | bytes 6148
  6.5 73.4 %copy-start = (bf16[512,1024]{1,0:T(8,128)(2,1)S(1)}, bf16[512,1024]{1,0:T(8,128)(2,1)}, u32[]{:S(2)}) copy-start(bf16[512,1024]{1,0:T(8,128)(2,1)} %param.10) | copy-start | bytes 3145732
  6.5 73.7 %copy-start.8 = (f32[2,16]{1,0:T(2,128)S(1)}, f32[2,16]{1,0:T(2,128)}, u32[]{:S(2)}) copy-start(f32[2,16]{1,0:T(2,128)} %param.14) | copy-start | bytes 388
  6.5 73.7 %copy-start.6 = (f32[2,1024]{1,0:T(2,128)S(1)}, f32[2,1024]{1,0:T(2,128)}, u32[]{:S(2)}) copy-start(f32[2,1024]{1,0:T(2,128)} %param.11) | copy-start | bytes 24580
  6.5 74.1 %copy-start.5 = (s32[512]{0:T(512)S(1)}, s32[512]{0:T(512)}, u32[]{:S(2)}) copy-start(s32[512]{0:T(512)} %param.17) | copy-start | bytes 6148
  6.6 74.1 %copy-start.4 = (s32[512]{0:T(512)S(1)}, s32[512]{0:T(512)}, u32[]{:S(2)}) copy-start(s32[512]{0:T(512)} %param.18) | copy-start | bytes 6148
  6.6 50.3 %all-gather.10.cloned.1.call-start = ((), (), s32[]{:S(2)}) async-start(), calls=%async_computation.2 | async-start | bytes 1802240 | tf_op jit(solution)/shard_map/all_gather | solution.py:102
  8.8 94.8 %all-gather.6.cloned.1.call-start = ((), (), s32[]{:S(2)}) async-start(), calls=%async_computation | async-start | bytes 7077888 | tf_op jit(solution)/shard_map/all_gather | solution.py:87
  36.6 104.8 %all-gather.8.cloned.1.call-start = ((), (), s32[]{:S(2)}) async-start(), calls=%async_computation.1 | async-start | bytes 2359296 | tf_op jit(solution)/shard_map/all_gather | solution.py:97
  55.7 147.3 %all-gather.12.cloned.1.call-start = ((), (), s32[]{:S(2)}) async-start(), calls=%async_computation.3 | async-start | bytes 12976128 | tf_op jit(solution)/shard_map/all_gather | solution.py:107
  61.8 187.2 %all-gather.14.cloned.1.call-start = ((), (), s32[]{:S(2)}) async-start(), calls=%async_computation.4 | async-start | bytes 6488064 | tf_op jit(solution)/shard_map/all_gather | solution.py:114
  121.3 9.0 %copy-start.2 = (bf16[1,512,1024]{1,2,0:T(8,128)(2,1)S(1)}, bf16[1,512,1024]{1,2,0:T(8,128)(2,1)}, u32[]{:S(2)}) copy-start(bf16[1,512,1024]{1,2,0:T(8,128)(2,1)} %copy.23) | copy-start | bytes 3145732
  130.3 11.1 %copy-start.1 = (bf16[512,1024]{1,0:T(8,128)(2,1)S(1)}, bf16[512,1024]{1,0:T(8,128)(2,1)}, u32[]{:S(2)}) copy-start(bf16[512,1024]{1,0:T(8,128)(2,1)} %param.10) | copy-start | bytes 3145732
Sparse Core Ops, SparseCore 0:
  8.9 47.8 all-gather.9
  58.8 44.7 all-gather.5
  105.5 28.0 all-gather.7
  135.4 67.5 all-gather.11
  204.7 44.2 all-gather.13

commit v2 on v1

--- a/solution.py
+++ b/solution.py
@@ -1,6 +1,11 @@
+import functools
+import math
+
 import jax
 import jax.numpy as jnp
 from jax import lax
+from jax.experimental import pallas as pl
+from jax.experimental.pallas import tpu as pltpu
 from jax.sharding import PartitionSpec as P
 
 HEAD_DIM = 64
@@ -116,10 +121,339 @@
     )
     return (residual.astype(jnp.float32) + feed).astype(jnp.bfloat16)
 
+MESH = pl.DeviceIdType.MESH
+PIECES = 4
+ROWS = 256
+WIDE = 2 * HEAD_DIM
+
+
+def event_order(spans):
+    due = []
+    start = 0.0
+    for which, span in enumerate(spans):
+        begin = max(0.0, start - 0.12 * sum(spans))
+        for stage, part in enumerate((0.0, 0.15, 0.3, 0.55, 0.8, 1.0)):
+            due.append((begin + part * 1.3 * span, which, stage))
+        start += span
+    return [(which, stage) for _, which, stage in sorted(due)]
+
+
+def layer_kernel(
+    ring, spans,
+    bias_ref, tokens_ref, gain_ref, ids_ref, qkv_in, out_in, ffn_in, down_in,
+    final_ref,
+    qkv_buf, out_buf, gate_buf, up_buf, down_buf,
+    normed, queries, keys, values, attended, residual, gates, hidden, cosine, sine, columns,
+    send_sem, recv_sem, local_sem,
+):
+    bufs = (qkv_buf, out_buf, gate_buf, up_buf, down_buf)
+    dp = lax.axis_index("dp")
+    z = lax.axis_index("mp")
+    core = lax.rem(dp, 2)
+    x = lax.rem(dp // 2, 2)
+    y = dp // 4
+    up_z = lax.rem(z + 1, ring)
+    down_z = lax.rem(z + ring - 1, ring)
+    whole = slice(None)
+    to_x = {"dp": (y * 2 + 1 - x) * 2 + core, "mp": z}
+    to_y = {"dp": ((1 - y) * 2 + x) * 2 + core, "mp": z}
+    to_core = {"dp": (y * 2 + x) * 2 + 1 - core, "mp": z}
+    to_up = {"dp": dp, "mp": up_z}
+    to_down = {"dp": dp, "mp": down_z}
+
+    def target(piece, hop):
+        mirrored = piece % 2 == 1
+        if hop == 0:
+            return to_up
+        if hop == 1:
+            return to_down
+        if hop == 2:
+            return to_down if mirrored else to_up
+        if hop == 3:
+            return to_y if mirrored else to_x
+        if hop == 4:
+            return to_x if mirrored else to_y
+        return to_core
+
+    def region(piece, hop):
+        mirrored = piece % 2 == 1
+        behind = up_z if mirrored else down_z
+        pair = (whole, x) if mirrored else (y, whole)
+        if hop == 5:
+            return (whole, whole, core, whole)
+        if piece < 2:
+            return {
+                0: (y, x, core, z), 1: (y, x, core, z), 2: (y, x, core, behind),
+                3: (y, x, core, whole), 4: pair + (core, whole),
+            }[hop]
+        return {
+            3: (y, x, core, z), 4: pair + (core, z), 0: (whole, whole, core, z),
+            1: (whole, whole, core, z), 2: (whole, whole, core, behind),
+        }[hop]
+
+    def copy(which, piece, hop):
+        part = bufs[which].at[region(piece, hop) + (whole, piece)]
+        slot = (which * PIECES + piece) * 6 + hop
+        return pltpu.make_async_remote_copy(
+            src_ref=part, dst_ref=part, send_sem=send_sem.at[slot], recv_sem=recv_sem.at[slot],
+            device_id=target(piece, hop), device_id_type=MESH,
+        )
+
+    def own(which):
+        source = (qkv_in, out_in, ffn_in.at[pl.ds(0, 1)], ffn_in.at[pl.ds(1, 1)], down_in)[which]
+        return pltpu.make_async_copy(source, bufs[which].at[y, x, core, z], local_sem.at[which])
+
+    def event(which, stage):
+        for piece in range(PIECES):
+            early = piece < 2
+            first, second = (1, 0) if piece % 2 else (0, 1)
+            waits, sends = (
+                (((), (0, 1)), ((first,), (2,)), ((second, 2), (3,)), ((3,), (4,)), ((4,), (5,)), ((5,), ()))
+                if early else
+                (((), (3,)), ((3,), (4,)), ((4,), (0, 1)), ((first,), (2,)), ((second, 2), (5,)), ((5,), ()))
+            )[stage]
+            for hop in waits:
+                copy(which, piece, hop).wait_recv()
+            for hop in sends:
+                copy(which, piece, hop).start()
+
+    order = event_order(spans)
+    cursor = [0]
+
+    def take(count):
+        picked = order[cursor[0]:cursor[0] + count]
+        cursor[0] += len(picked)
+        return picked
+
+    def until(which):
+        return take(order.index((which, 5)) + 1 - cursor[0])
+
+    def at_steps(total, picked):
+        plan = [[] for _ in range(total)]
+        for place, item in enumerate(picked):
+            plan[place * total // len(picked)].append(item)
+
+        def run(step):
+            for place, items in enumerate(plan):
+                if items:
+                    @pl.when(step == place)
+                    def _():
+                        for item in items:
+                            event(*item)
+        return run
+
+    for which in range(len(bufs)):
+        own(which).start()
+    barrier = pltpu.get_barrier_semaphore()
+    for peer in (to_x, to_y, to_core, to_up, to_down):
+        pl.semaphore_signal(barrier, inc=1, device_id=peer, device_id_type=MESH)
+    pl.semaphore_wait(barrier, 5)
+    for which in range(len(bufs)):
+        own(which).wait()
+
+    first_wave = until(0)
+    cut = min(3, len(first_wave))
+    for item in first_wave[:cut]:
+        event(*item)
+
+    total_rows, width = tokens_ref.shape
+    blocks = total_rows // ROWS
+
+    def norm_rows(source, gain_row):
+        gain = gain_ref[gain_row:gain_row + 1, :]
+
+        def body(step, carry):
+            rows = pl.ds(pl.multiple_of(step * 128, 128), 128)
+            wide = source[rows, :].astype(jnp.float32)
+            square = jnp.mean(wide * wide, axis=-1, keepdims=True)
+            normed[rows, :] = (wide * lax.rsqrt(square + 1e-05) * gain).astype(jnp.bfloat16)
+            return carry
+        lax.fori_loop(0, total_rows // 128, body, 0)
+
+    norm_rows(tokens_ref, 0)
+    ids = ids_ref[...].astype(jnp.float32)
+    times = jnp.broadcast_to(ids[2:3, :], (WIDE, total_rows)).T
+    columns[0] = jnp.broadcast_to(ids[0:1, :], (WIDE, total_rows)).T
+    columns[1] = jnp.broadcast_to(ids[1:2, :], (WIDE, total_rows)).T
+    half = HEAD_DIM // 2
+    lane = lax.broadcasted_iota(jnp.int32, (1, WIDE), 1)
+    slot_in_half = lax.rem(lane, half).astype(jnp.float32)
+    freq = jnp.exp(slot_in_half * (-math.log(10000.0) / half))
+    front = lax.rem(lane, HEAD_DIM) < half
+    angle = times * freq
+    cosine[...] = jnp.cos(angle)
+    sine[...] = jnp.where(front, -1.0, 1.0) * jnp.sin(angle)
+
+    for item in first_wave[cut:]:
+        event(*item)
+
+    def rotated_wide(raw):
+        swapped = jnp.where(front, pltpu.roll(raw, WIDE - half, 1), pltpu.roll(raw, half, 1))
+        return raw * cosine[...] + swapped * sine[...]
+
+    later = until(2)
+    early_count = min(len(later), 3)
+    project_events = at_steps(ring, later[:early_count])
+    attend_steps = (width // WIDE) * blocks
+    attend_events = at_steps(attend_steps, later[early_count:])
+
+    def project(step, carry):
+        def product(kind):
+            shape = (width, qkv_buf.shape[-1])
+            weight = qkv_buf[:, :, :, step, kind].reshape(shape)
+            return jnp.dot(normed[...], weight, preferred_element_type=jnp.float32)
+        groups = qkv_buf.shape[-1] // WIDE
+        for kind, held in enumerate((queries, keys, values)):
+            raw = product(kind)
+            for group in range(groups):
+                part = raw[:, group * WIDE:(group + 1) * WIDE]
+                if kind < 2:
+                    part = rotated_wide(part)
+                part = part.astype(jnp.bfloat16)
+                if kind == 0:
+                    part = part * jnp.bfloat16(HEAD_DIM ** -0.5)
+                held[step * groups + group] = part
+        project_events(step)
+        return carry
+    lax.fori_loop(0, ring, project, 0)
+
+    left = lane < HEAD_DIM
+
+    def attend_step(step, carry):
+        pair = step // blocks
+        block = lax.rem(step, blocks)
+        rows = pl.ds(pl.multiple_of(block * ROWS, ROWS), ROWS)
+        base = pl.multiple_of((block * ROWS) // L * L, L)
+        span = pl.ds(base, L)
+        same_series = columns[0, rows, 0:1] == ids_ref[0:1, span].astype(jnp.float32)
+        same_variate = columns[1, rows, 0:1] == ids_ref[1:2, span].astype(jnp.float32)
+        both = queries[pair, rows, :]
+        key_rows = keys[pair, span, :]
+        value_rows = values[pair, span, :]
+        results = []
+        for side in range(2):
+            head = pair * 2 + side
+            chosen = left if side == 0 else jnp.logical_not(left)
+            mine = both * chosen.astype(jnp.bfloat16)
+            scores = lax.dot_general(
+                mine, key_rows, (((1,), (1,)), ((), ())), preferred_element_type=jnp.float32
+            )
+            scores = scores + jnp.where(same_variate, bias_ref[0, head], bias_ref[1, head])
+            scores = jnp.where(same_series, scores, -1e30)
+            top = jnp.max(scores, axis=1, keepdims=True)
+            expo = jnp.exp(scores - top)
+            total = jnp.sum(expo, axis=1, keepdims=True)
+            mixed = jnp.dot(
+                expo.astype(jnp.bfloat16), value_rows, preferred_element_type=jnp.float32
+            )
+            results.append(mixed / total)
+        lanes = pl.ds(pl.multiple_of(pair * WIDE, WIDE), WIDE)
+        attended[rows, lanes] = jnp.where(left, results[0], results[1]).astype(jnp.bfloat16)
+        attend_events(step)
+        return carry
+    lax.fori_loop(0, attend_steps, attend_step, 0)
+
+    def block_pair(buf, side_y, side_x, index):
+        return jnp.concatenate(
+            [buf[side_y, side_x, half_core, index].reshape(-1, buf.shape[-1]) for half_core in range(2)],
+            axis=1,
+        )
+
+    slab = 2 * out_buf.shape[-1]
+
+    def out_step(step, carry):
+        lanes = pl.ds(pl.multiple_of(step * slab, slab), slab)
+        weight = block_pair(out_buf, step // 2, lax.rem(step, 2), whole)
+        mixed = jnp.dot(attended[...], weight, preferred_element_type=jnp.float32)
+        residual[:, lanes] = (tokens_ref[:, lanes].astype(jnp.float32) + mixed).astype(jnp.bfloat16)
+        return carry
+    lax.fori_loop(0, 4, out_step, 0)
+    norm_rows(residual, 1)
+
+    gate_events = at_steps(ring, until(3))
+
+    def gate_step(step, carry):
+        weight = gate_buf[:, :, :, step].reshape(width, gate_buf.shape[-1])
+        gates[step] = jnp.dot(normed[...], weight, preferred_element_type=jnp.float32)
+        gate_events(step)
+        return carry
+    lax.fori_loop(0, ring, gate_step, 0)
+
+    up_events = at_steps(ring, until(4))
+
+    def up_step(step, carry):
+        weight = up_buf[:, :, :, step].reshape(width, up_buf.shape[-1])
+        up = jnp.dot(normed[...], weight, preferred_element_type=jnp.float32)
+        gate = gates[step]
+        hidden[step] = (gate / (1.0 + jnp.exp(-gate)) * up).astype(jnp.bfloat16)
+        up_events(step)
+        return carry
+    lax.fori_loop(0, ring, up_step, 0)
+
+    def down_step(step, carry):
+        lanes = pl.ds(pl.multiple_of(step * slab, slab), slab)
+        total = residual[:, lanes].astype(jnp.float32)
+        for index in range(ring):
+            weight = block_pair(down_buf, step // 2, lax.rem(step, 2), index)
+            total = total + jnp.dot(hidden[index], weight, preferred_element_type=jnp.float32)
+        final_ref[:, lanes] = total.astype(jnp.bfloat16)
+        return carry
+    lax.fori_loop(0, 4, down_step, 0)
+
+    def drain(which, piece, hop):
+        copy(which, piece, hop).wait_send()
+    for which in range(len(bufs)):
+        for piece in range(PIECES):
+            for hop in range(6):
+                drain(which, piece, hop)
+
+
+def fused(
+    ring, tokens, norm_gain, qkv_weight, out_weight, variate_bias, ffn_weight, down_weight,
+    sample_ids, variate_ids, time_ids,
+):
+    rows, width = tokens.shape
+    ids = jnp.stack([sample_ids, variate_ids, time_ids])
+    qkv = qkv_weight.reshape(qkv_weight.shape[0], PIECES, -1, qkv_weight.shape[2])
+    out = out_weight.reshape(1, PIECES, -1, out_weight.shape[1])
+    ffn = ffn_weight.reshape(2, PIECES, -1, ffn_weight.shape[2])
+    down = down_weight.reshape(1, PIECES, -1, down_weight.shape[1])
+    spans = tuple(float(n) for n in (qkv.size, out.size, ffn.size // 2, ffn.size // 2, down.size))
+    shapes = (qkv.shape, out.shape, (1,) + ffn.shape[1:], (1,) + ffn.shape[1:], down.shape)
+    buffers = [pltpu.VMEM((2, 2, 2, ring) + shape, jnp.bfloat16) for shape in shapes]
+    pairs = width // WIDE
+    per_pair = pltpu.VMEM((pairs, rows, WIDE), jnp.bfloat16)
+    flat = pltpu.VMEM((rows, width), jnp.bfloat16)
+    vmem = pl.BlockSpec(memory_space=pltpu.VMEM)
+    anywhere = pl.BlockSpec(memory_space=pl.ANY)
+    copies = len(shapes) * PIECES * 6
+    return pl.pallas_call(
+        functools.partial(layer_kernel, ring, spans),
+        out_shape=jax.ShapeDtypeStruct((rows, width), jnp.bfloat16),
+        in_specs=[pl.BlockSpec(memory_space=pltpu.SMEM), vmem, vmem, vmem] + [anywhere] * 4,
+        out_specs=vmem,
+        scratch_shapes=buffers + [
+            flat, per_pair, per_pair, per_pair, flat, flat,
+            pltpu.VMEM((ring, rows, ffn.shape[-1]), jnp.float32),
+            pltpu.VMEM((ring, rows, ffn.shape[-1]), jnp.bfloat16),
+            pltpu.VMEM((rows, WIDE), jnp.float32),
+            pltpu.VMEM((rows, WIDE), jnp.float32),
+            pltpu.VMEM((2, rows, WIDE), jnp.float32),
+            pltpu.SemaphoreType.DMA((copies,)),
+            pltpu.SemaphoreType.DMA((copies,)),
+            pltpu.SemaphoreType.DMA((len(shapes),)),
+        ],
+        compiler_params=pltpu.CompilerParams(
+            collective_id=0, has_side_effects=True, vmem_limit_bytes=60 * 1024 * 1024
+        ),
+    )(variate_bias, tokens, norm_gain, ids, qkv, out, ffn, down)
+
 
 def solution(mesh):
+    ring = mesh.shape["mp"]
+    body = functools.partial(fused, ring) if (mesh.shape["dp"], ring) == (2 ** 3, 2 ** 2) else local
     return jax.shard_map(
-        local,
+        body,
         mesh=mesh,
         in_specs=(
             P(("dp", "mp"), None),

time: 266 us -> 186 us (0.70)
  Pallas kernels: 0 us -> 179 us
  waiting for transfers between devices: 114 us -> 0 us
  blocking collectives: 64.8 us -> 0 us
  matrix products: 53 us -> 0 us
  between operations: 13.3 us -> 0.01 us
  local copies, waits for them, and re-layouts: 15.9 us -> 4.88 us
  other arithmetic: 4.88 us -> 0.61 us
    pallas_call x0 -> x1, Pallas kernels: none -> 179 us  [fused(): pl.pallas_call(functools.partial(layer_kernel, ring, spans), out_shape=ja...]
    all_gather x5 -> x0, waiting for transfers between devices: 114 us -> none  [the longest x1 57.8 us: local(): lax.all_gather(ffn_columns, 'dp', axis=1, tiled=True)]
    all_gather x3 -> x0, blocking collectives: 64.8 us -> none  [the longest x1 27.7 us: local(): wide_columns = lax.all_gather(qkv_weight, 'mp', axis=2, tiled=True)]
    dot_general x5 -> x0, matrix products: 44 us -> none  [the longest x1 13.3 us: local(): jnp.einsum('rc,jcf->jrf', columns, lax.all_gather(ffn_columns, 'dp', axis...]
    sub x1 -> x0, matrix products: 8.99 us -> none  [one_sequence(): expo = jnp.exp(scores - top)]
    slice x6 -> x0, local copies, waits for them, and re-layouts: 8.79 us -> none  [the longest x2 4.38 us: local(): queries = rotated(projected[0], time_ids)]
    all_gather x1 -> x0, local copies, waits for them, and re-layouts: 4.91 us -> none  [local(): ffn_columns = lax.all_gather(ffn_weight, 'mp', axis=2, tiled=True)]
  transfers between devices with their start and end apart: 5 -> 0, of which waited for: 4 -> 0; matrix products, arithmetic and copies ran while one was open for 23% -> 0% of each run, Pallas kernels for 0% -> 0%
where the time goes in v2:
time: 186 us; the launch traced here: 184 us
  Pallas kernels  179 us (96%)
  local copies, waits for them, and re-layouts  4.88 us (3%)
    pallas_call x1, Pallas kernels, fused(): pl.pallas_call(functools.partial(layer_kernel, ring, spans), out_shape=ja...  179 us
    unnamed x8, local copies, waits for them, and re-layouts  4.88 us

profile of v2, /device:TPU:0, one launch (start us, length us, event | category | flops | bytes accessed | tf_op | source)
XLA Modules:
  0.0 184.0 jit_solution(8962740998989998041)
XLA Ops:
  0.0 0.0 copy-start.2
  0.0 0.0 copy-start.1
  0.0 0.0 copy-start
  0.0 0.7 copy-done.2
  0.7 0.0 copy-done.1
  0.7 0.0 copy-done
  0.7 0.6 pad_add_fusion.ids_ref
  1.3 1.9 %copy.11 = bf16[2,128,704]{2,1,0:T(8,128)(2,1)} copy(bf16[2,128,704]{1,2,0:T(8,128)(2,1)} %param.15) | data formatting | bytes 720896 | tf_op args[5]
  3.2 178.5 %shard_map.100 = bf16[512,1024]{1,0:T(8,128)(2,1)} custom-call(f32[2,16]{1,0:T(2,128)} %bias_ref.1, bf16[512,1024]{1,0:T(8,128)(2,1)} %tokens_ref.1, f32[2,1024]{1,0:T(2,128)} %gain_ref.1, s32[3,512]{1,0:T(4,128)} %pad_add_fusion.ids_ref, bf16[3,4,32,256]{3,2,1,0:T(8,128)(2,1)} %bitcast.8, bf16[1,4,64,128]{3,2,1,0:T(8,128)(2,1)} %bitcast.10, ...), custom_call_target="tpu_custom_call" | custom-call | tf_op jit(solution)/shard_map/pallas_call | solution.py:430
  181.8 2.3 %copy.13 = bf16[512,1024]{1,0:T(8,128)(2,1)} copy(bf16[512,1024]{1,0:T(8,128)(2,1)} %shard_map.100) | data formatting | bytes 2097152
Async XLA Ops:
  0.0 0.7 copy-start.2
  0.0 0.7 copy-start.1
  0.0 0.7 copy-start

commit v3 on v2

--- a/solution.py
+++ b/solution.py
@@ -125,21 +125,22 @@
 PIECES = 4
 ROWS = 256
 WIDE = 2 * HEAD_DIM
-
-
-def event_order(spans):
+STAGES = 7
+ARRAY_TURNS = 1.5
+LATE_TURNS = 1.2
+
+
+def event_order(arrays):
     due = []
-    start = 0.0
-    for which, span in enumerate(spans):
-        begin = max(0.0, start - 0.12 * sum(spans))
-        for stage, part in enumerate((0.0, 0.15, 0.3, 0.55, 0.8, 1.0)):
-            due.append((begin + part * 1.3 * span, which, stage))
-        start += span
-    return [(which, stage) for _, which, stage in sorted(due)]
+    for which in range(arrays):
+        for stage in range(STAGES):
+            for late in range(2):
+                due.append((which * ARRAY_TURNS + stage + late * LATE_TURNS, which, stage, late))
+    return [item[1:] for item in sorted(due)]
 
 
 def layer_kernel(
-    ring, spans,
+    ring,
     bias_ref, tokens_ref, gain_ref, ids_ref, qkv_in, out_in, ffn_in, down_in,
     final_ref,
     qkv_buf, out_buf, gate_buf, up_buf, down_buf,
@@ -160,64 +161,98 @@
     to_core = {"dp": (y * 2 + x) * 2 + 1 - core, "mp": z}
     to_up = {"dp": dp, "mp": up_z}
     to_down = {"dp": dp, "mp": down_z}
-
-    def target(piece, hop):
-        mirrored = piece % 2 == 1
-        if hop == 0:
+    steps = ring - 1
+    first_pair, second_pair, across = 2 * steps, 2 * steps + 1, 2 * steps + 2
+    hops = 2 * steps + 3
+
+    def x_leads(which, piece):
+        return (which + piece) % 2 == 0
+
+    def z_leads(piece):
+        return piece < PIECES - 1
+
+    def target(which, piece, hop):
+        if hop < steps:
             return to_up
-        if hop == 1:
+        if hop < 2 * steps:
             return to_down
-        if hop == 2:
-            return to_down if mirrored else to_up
-        if hop == 3:
-            return to_y if mirrored else to_x
-        if hop == 4:
-            return to_x if mirrored else to_y
-        return to_core
-
-    def region(piece, hop):
-        mirrored = piece % 2 == 1
-        behind = up_z if mirrored else down_z
-        pair = (whole, x) if mirrored else (y, whole)
-        if hop == 5:
+        if hop == across:
+            return to_core
+        return to_x if (hop == first_pair) == x_leads(which, piece) else to_y
+
+    def region(which, piece, hop):
+        pair = (y, whole) if x_leads(which, piece) else (whole, x)
+        if hop == across:
             return (whole, whole, core, whole)
-        if piece < 2:
-            return {
-                0: (y, x, core, z), 1: (y, x, core, z), 2: (y, x, core, behind),
-                3: (y, x, core, whole), 4: pair + (core, whole),
-            }[hop]
-        return {
-            3: (y, x, core, z), 4: pair + (core, z), 0: (whole, whole, core, z),
-            1: (whole, whole, core, z), 2: (whole, whole, core, behind),
-        }[hop]
-
-    def copy(which, piece, hop):
-        part = bufs[which].at[region(piece, hop) + (whole, piece)]
-        slot = (which * PIECES + piece) * 6 + hop
+        if hop == first_pair:
+            return (y, x, core, whole if z_leads(piece) else z)
+        if hop == second_pair:
+            return pair + (core, whole if z_leads(piece) else z)
+        block = z - hop if hop < steps else z + (hop - steps)
+        return ((y, x) if z_leads(piece) else (whole, whole)) + (core, block)
+
+    def sends_now(hop):
+        if hop < steps:
+            return jnp.logical_and(z >= hop, z < ring - 1)
+        return jnp.logical_and(z + (hop - steps) < ring, z > 0)
+
+    def lands_now(hop):
+        if hop < steps:
+            return z >= hop + 1
+        return z + (hop - steps) + 1 < ring
+
+    def copy(which, piece, hop, fixed=False):
+        at = region(which, piece, hop)
+        if fixed and hop < 2 * steps:
+            at = at[:3] + (z,)
+        part = bufs[which].at[at + (whole, piece)]
+        slot = (which * PIECES + piece) * hops + hop
         return pltpu.make_async_remote_copy(
             src_ref=part, dst_ref=part, send_sem=send_sem.at[slot], recv_sem=recv_sem.at[slot],
-            device_id=target(piece, hop), device_id_type=MESH,
+            device_id=target(which, piece, hop), device_id_type=MESH,
         )
+
+    def guarded(hop, condition, action):
+        if hop < 2 * steps:
+            pl.when(condition(hop))(action)
+        else:
+            action()
+
+    def send(which, piece, hop):
+        guarded(hop, sends_now, lambda: copy(which, piece, hop).start())
+
+    def land(which, piece, hop):
+        guarded(hop, lands_now, lambda: copy(which, piece, hop, True).wait_recv())
+
+    def sent(which, piece, hop):
+        guarded(hop, sends_now, lambda: copy(which, piece, hop, True).wait_send())
 
     def own(which):
         source = (qkv_in, out_in, ffn_in.at[pl.ds(0, 1)], ffn_in.at[pl.ds(1, 1)], down_in)[which]
         return pltpu.make_async_copy(source, bufs[which].at[y, x, core, z], local_sem.at[which])
 
-    def event(which, stage):
+    line = [((), (0, steps))]
+    for step in range(1, steps):
+        line.append(((step - 1, steps + step - 1), (step, steps + step)))
+    line_end = (steps - 1, 2 * steps - 1)
+    z_first = line + [
+        (line_end, (first_pair,)), ((first_pair,), (second_pair,)), ((second_pair,), (across,)),
+        ((across,), ()),
+    ]
+    z_last = [((), (first_pair,)), ((first_pair,), (second_pair,)), ((second_pair,), line[0][1])]
+    z_last += line[1:] + [(line_end, (across,)), ((across,), ())]
+
+    def event(which, stage, late):
         for piece in range(PIECES):
-            early = piece < 2
-            first, second = (1, 0) if piece % 2 else (0, 1)
-            waits, sends = (
-                (((), (0, 1)), ((first,), (2,)), ((second, 2), (3,)), ((3,), (4,)), ((4,), (5,)), ((5,), ()))
-                if early else
-                (((), (3,)), ((3,), (4,)), ((4,), (0, 1)), ((first,), (2,)), ((second, 2), (5,)), ((5,), ()))
-            )[stage]
+            if z_leads(piece) == bool(late):
+                continue
+            waits, sends = (z_first if z_leads(piece) else z_last)[stage]
             for hop in waits:
-                copy(which, piece, hop).wait_recv()
+                land(which, piece, hop)
             for hop in sends:
-                copy(which, piece, hop).start()
-
-    order = event_order(spans)
+                send(which, piece, hop)
+
+    order = event_order(len(bufs))
     cursor = [0]
 
     def take(count):
@@ -226,7 +261,8 @@
         return picked
 
     def until(which):
-        return take(order.index((which, 5)) + 1 - cursor[0])
+        ends = [order.index((which, STAGES - 1, late)) for late in range(2)]
+        return take(max(ends) + 1 - cursor[0])
 
     def at_steps(total, picked):
         plan = [[] for _ in range(total)]
@@ -400,12 +436,10 @@
         return carry
     lax.fori_loop(0, 4, down_step, 0)
 
-    def drain(which, piece, hop):
-        copy(which, piece, hop).wait_send()
     for which in range(len(bufs)):
         for piece in range(PIECES):
-            for hop in range(6):
-                drain(which, piece, hop)
+            for hop in range(hops):
+                sent(which, piece, hop)
 
 
 def fused(
@@ -418,7 +452,6 @@
     out = out_weight.reshape(1, PIECES, -1, out_weight.shape[1])
     ffn = ffn_weight.reshape(2, PIECES, -1, ffn_weight.shape[2])
     down = down_weight.reshape(1, PIECES, -1, down_weight.shape[1])
-    spans = tuple(float(n) for n in (qkv.size, out.size, ffn.size // 2, ffn.size // 2, down.size))
     shapes = (qkv.shape, out.shape, (1,) + ffn.shape[1:], (1,) + ffn.shape[1:], down.shape)
     buffers = [pltpu.VMEM((2, 2, 2, ring) + shape, jnp.bfloat16) for shape in shapes]
     pairs = width // WIDE
@@ -426,9 +459,9 @@
     flat = pltpu.VMEM((rows, width), jnp.bfloat16)
     vmem = pl.BlockSpec(memory_space=pltpu.VMEM)
     anywhere = pl.BlockSpec(memory_space=pl.ANY)
-    copies = len(shapes) * PIECES * 6
+    copies = len(shapes) * PIECES * (2 * ring + 1)
     return pl.pallas_call(
-        functools.partial(layer_kernel, ring, spans),
+        functools.partial(layer_kernel, ring),
         out_shape=jax.ShapeDtypeStruct((rows, width), jnp.bfloat16),
         in_specs=[pl.BlockSpec(memory_space=pltpu.SMEM), vmem, vmem, vmem] + [anywhere] * 4,
         out_specs=vmem,

time: 186 us -> 135 us (0.73)
  Pallas kernels: 179 us -> 128 us
    pallas_call x1, Pallas kernels: 179 us -> 128 us  [fused(): pl.pallas_call(functools.partial(layer_kernel, ring), out_shape=jax.Shape...]
where the time goes in v3:
time: 135 us; the launch traced here: 134 us
  Pallas kernels  128 us (95%)
  local copies, waits for them, and re-layouts  4.88 us (4%)
    pallas_call x1, Pallas kernels, fused(): pl.pallas_call(functools.partial(layer_kernel, ring), out_shape=jax.Shape...  128 us
    unnamed x8, local copies, waits for them, and re-layouts  4.88 us

profile of v3, /device:TPU:0, one launch (start us, length us, event | category | flops | bytes accessed | tf_op | source)
XLA Modules:
  0.0 133.8 jit_solution(7722464569115222224)
XLA Ops:
  0.0 0.0 copy-start.2
  0.0 0.0 copy-start.1
  0.0 0.0 copy-start
  0.0 0.7 copy-done.2
  0.7 0.0 copy-done.1
  0.7 0.0 copy-done
  0.7 0.6 pad_add_fusion.ids_ref
  1.3 1.9 %copy.11 = bf16[2,128,704]{2,1,0:T(8,128)(2,1)} copy(bf16[2,128,704]{1,2,0:T(8,128)(2,1)} %param.15) | data formatting | bytes 720896 | tf_op args[5]
  3.2 128.3 %shard_map.100 = bf16[512,1024]{1,0:T(8,128)(2,1)} custom-call(f32[2,16]{1,0:T(2,128)} %bias_ref.1, bf16[512,1024]{1,0:T(8,128)(2,1)} %tokens_ref.1, f32[2,1024]{1,0:T(2,128)} %gain_ref.1, s32[3,512]{1,0:T(4,128)} %pad_add_fusion.ids_ref, bf16[3,4,32,256]{3,2,1,0:T(8,128)(2,1)} %bitcast.8, bf16[1,4,64,128]{3,2,1,0:T(8,128)(2,1)} %bitcast.10, ...), custom_call_target="tpu_custom_call" | custom-call | tf_op jit(solution)/shard_map/pallas_call | solution.py:463
  131.5 2.3 %copy.13 = bf16[512,1024]{1,0:T(8,128)(2,1)} copy(bf16[512,1024]{1,0:T(8,128)(2,1)} %shard_map.100) | data formatting | bytes 2097152
Async XLA Ops:
  0.0 0.7 copy-start.2
  0.0 0.7 copy-start.1
  0.0 0.7 copy-start
